TPU v7x, 32 devices: a whole 2x2x4 slice. The times are simulated.
32 devices in a mesh: chip: 2 (over y), board: 4 (over z), cuts: 4 (over x, core).
Axes of the slice: x: 2, y: 2, z: 4, core: 2. Of those that a mesh axis runs over, the one named last changes fastest.
Arguments:
- features: bfloat16 [32, 2048, 1024], P(('chip', 'board', 'cuts')), may hold values from -6 to 6
- targets: bfloat16 [32, 2048, 256], P(('chip', 'board', 'cuts')), may hold values from -24 to 24
- lower_weight: bfloat16 [32, 1024, 512], P(('chip', 'board', 'cuts')), may hold values from -0.1875 to 0.1875
- head_weight: float32 [32, 512, 256], P(('chip', 'board', 'cuts')), may hold values from -0.25 to 0.25
- batch_rows: int32 [32, 2, 1024], P(('chip', 'board', 'cuts')), may hold values from 0 to 2047
- sample_counts: int32 [32], P(('chip', 'board', 'cuts')), may hold values from 1 to 1000
- cluster_ids: int32 [32], P(('chip', 'board', 'cuts')), may hold values from 0 to 7, as said below
Outputs:
- cluster_step: float32 [32, 512, 256], P(('chip', 'board', 'cuts'))
Inputs may be any that keep to these rules, and one draw needn't show every extreme that they name: `cluster_ids`: every one of the 8 clusters has at least one client.
All inputs are finite; a program needn't handle non-finite values.
Results may differ from a plain program's by a relative error of at most 0.0003.
Values sent between devices are 32-bit elements; how exact they have to be, the bound alone decides.
No kernel may reach another device: no remote copies, remote signals or barrier semaphores. Data moves between devices by JAX's collectives and lax.ppermute only.
A program may use at most 64 MiB of HBM per device.

v0:
```python
import jax
import jax.numpy as jnp
from jax import lax
from jax.sharding import PartitionSpec as P

LR = 0.5


def on_device(features, targets, lower_weight, head_weight, batch_rows, sample_counts, cluster_ids):
    hidden = jnp.tanh(jnp.dot(features[0], lower_weight[0], preferred_element_type=jnp.float32))
    start = head_weight[0]
    weight = start
    count_rows = batch_rows.shape[2]
    for step in range(batch_rows.shape[1]):
        picked = jnp.take(hidden, batch_rows[0, step], axis=0)
        wanted = jnp.take(targets[0], batch_rows[0, step], axis=0).astype(jnp.float32)
        err = jnp.dot(picked, weight, precision=lax.Precision.HIGHEST) - wanted
        grad = jnp.dot(picked.T, err, precision=lax.Precision.HIGHEST) / count_rows
        weight = weight - LR * grad
    delta = weight - start
    cluster = cluster_ids[0]
    number = 8
    chip_count = lax.axis_size("chip")
    rest_count = lax.axis_size(("board", "cuts"))
    every_id, every_count = (
        lax.all_gather(cluster_ids, ("chip", "board", "cuts"), axis=0, tiled=True),
        lax.all_gather(sample_counts, ("chip", "board", "cuts"), axis=0, tiled=True),
    )
    table = (every_id[:, None] == jnp.arange(number, dtype=jnp.int32)[None, :]).astype(jnp.float32)
    weighted = table * every_count.astype(jnp.float32)[:, None]
    counts = jnp.sum(weighted, axis=0)
    scaled = (sample_counts[0].astype(jnp.float32) * delta).reshape(chip_count, rest_count, -1)
    columns = lax.all_to_all(
        lax.all_to_all(scaled, "chip", split_axis=0, concat_axis=0, tiled=True),
        ("board", "cuts"),
        split_axis=1,
        concat_axis=1,
        tiled=True,
    )
    columns = columns.reshape(chip_count * rest_count, -1)
    share = jnp.dot(table.T, columns, precision=lax.Precision.HIGHEST)
    outgoing = jnp.dot(table, share, precision=lax.Precision.HIGHEST)
    outgoing = outgoing.reshape(chip_count, rest_count, -1)
    arrived = lax.all_to_all(
        lax.all_to_all(outgoing, "chip", split_axis=0, concat_axis=0, tiled=True),
        ("board", "cuts"),
        split_axis=1,
        concat_axis=1,
        tiled=True,
    )
    mine = arrived.reshape(delta.shape)
    denom = lax.dynamic_index_in_dim(counts, cluster, 0, keepdims=False)
    return (mine / (LR * denom))[None]


def solution(mesh):
    return jax.shard_map(
        on_device,
        mesh=mesh,
        in_specs=(
            P(("chip", "board", "cuts"), None, None),
            P(("chip", "board", "cuts"), None, None),
            P(("chip", "board", "cuts"), None, None),
            P(("chip", "board", "cuts"), None, None),
            P(("chip", "board", "cuts"), None, None),
            P(("chip", "board", "cuts")),
            P(("chip", "board", "cuts")),
        ),
        out_specs=P(("chip", "board", "cuts"), None, None),
        check_vma=False,
    )
```

profile of v0, /device:TPU:0, one launch (start us, length us, event | category | flops | bytes accessed | tf_op | source)
XLA Modules:
  0.0 138.6 jit_solution(8541357281149164295)
XLA Ops:
  0.0 0.8 fusion.57
  0.8 0.4 copy-done
  1.3 6.5 %fusion.2 = f32[2048,512]{1,0:T(8,128)} fusion(bf16[1,2048,1024]{2,1,0:T(8,128)(2,1)} %param.11, bf16[1,1024,512]{2,1,0:T(8,128)(2,1)S(1)} %copy-done), kind=kOutput, calls=%fused_computation.6 | convolution fusion | flops 2147483648 | bytes 9437184 | tf_op jit(solution)/shard_map/dot_general | solution.py:10
  7.7 7.5 %gather_fusion = f32[1024,512]{1,0:T(8,128)} fusion(f32[2048,512]{1,0:T(8,128)} %fusion.2, s32[1024]{0:T(1024)S(1)} %fusion.49), kind=kCustom, calls=%fused_computation.clone | custom fusion | bytes 4198400 | tf_op jit(solution)/shard_map/jit(_take)/gather | solution.py:15
  15.3 5.0 %gather_fusion.1 = bf16[1024,256]{1,0:T(8,128)(2,1)} fusion(bf16[2048,256]{1,0:T(8,128)(2,1)S(1)} %bitcast.29, s32[1024]{0:T(1024)S(1)} %fusion.49), kind=kCustom, calls=%fused_computation.1.clone | custom fusion | bytes 1052672 | tf_op jit(solution)/shard_map/jit(_take)/gather | solution.py:16
  20.2 7.5 %gather_fusion.2 = f32[1024,512]{1,0:T(8,128)} fusion(f32[2048,512]{1,0:T(8,128)} %fusion.2, s32[1024]{0:T(1024)S(1)} %fusion.50), kind=kCustom, calls=%fused_computation.2.clone | custom fusion | bytes 4198400 | tf_op jit(solution)/shard_map/jit(_take)/gather | solution.py:15
  27.7 3.9 %gather_fusion.3 = bf16[1024,256]{1,0:T(8,128)(2,1)S(1)} fusion(bf16[2048,256]{1,0:T(8,128)(2,1)S(1)} %bitcast.30, s32[1024]{0:T(1024)S(1)} %fusion.50), kind=kCustom, calls=%fused_computation.3.clone | custom fusion | bytes 1052672 | tf_op jit(solution)/shard_map/jit(_take)/gather | solution.py:16
  31.7 3.7 %fusion.13 = f32[1024,256]{1,0:T(8,128)S(1)} fusion(f32[1024,512]{1,0:T(8,128)} %gather_fusion, pred[1024]{0:T(1024)(128)(4,1)S(1)} %compare_and_fusion.1, f32[1,512,256]{2,1,0:T(8,128)S(1)} %copy-done.4, bf16[1024,256]{1,0:T(8,128)(2,1)} %gather_fusion.1), kind=kOutput, calls=%fused_computation.15 | convolution fusion | flops 1611923456 | bytes 4195328 | tf_op jit(solution)/shard_map/dot_general | solution.py:17
  35.4 3.6 %fusion.34 = f32[512,256]{1,0:T(8,128)S(1)} fusion(f32[1024,256]{1,0:T(8,128)S(1)} %fusion.13, f32[1024,512]{1,0:T(8,128)S(1)} %copy-done.2, pred[1024]{0:T(1024)(128)(4,1)S(1)} %compare_and_fusion.1, f32[1,512,256]{2,1,0:T(8,128)S(1)} %copy-done.4), kind=kOutput, calls=%fused_computation.22 | convolution fusion | flops 1611399168 | bytes 4195328 | tf_op jit(solution)/shard_map/dot_general | solution.py:18
  39.7 2.4 %fusion.16 = f32[1024,256]{1,0:T(8,128)S(1)} fusion(f32[512,256]{1,0:T(8,128)S(1)} %fusion.34, f32[1024,512]{1,0:T(8,128)S(1)} %copy-done.3, pred[1024]{0:T(1024)(128)(4,1)S(1)} %compare_and_fusion, bf16[1024,256]{1,0:T(8,128)(2,1)S(1)} %gather_fusion.3), kind=kOutput, calls=%fused_computation.16 | convolution fusion | flops 1611923456 | bytes 4195328 | tf_op jit(solution)/shard_map/dot_general | solution.py:17
  42.1 3.6 %fusion.31 = f32[512,256]{1,0:T(8,128)S(1)} fusion(f32[512,256]{1,0:T(8,128)S(1)} %fusion.34, f32[1024,256]{1,0:T(8,128)S(1)} %fusion.16, f32[1024,512]{1,0:T(8,128)S(1)} %copy-done.3, pred[1024]{0:T(1024)(128)(4,1)S(1)} %compare_and_fusion, f32[1,512,256]{2,1,0:T(8,128)S(1)} %copy-done.4, f32[]{:T(128)} %bitcast), kind=kOutput, calls=%fused_computation.21 | convolution fusion | flops 1611661312 | bytes 4719620 | tf_op jit(solution)/shard_map/dot_general | solution.py:18
  45.9 12.1 %all_to_all.20 = f32[2,16,4096]{2,1,0:T(8,128)S(1)} all-to-all(f32[2,16,4096]{2,1,0:T(8,128)S(1)} %reshape.37), channel_id=1, replica_groups=mesh['chip'=2,'board'=4,'cuts'=4] {'chip'}, dimensions={0} | all-to-all | bytes 1048576 | tf_op jit(solution)/shard_map/all_to_all | solution.py:34
  58.0 1.2 copy.22
  59.2 5.9 %all-to-all-start.1 = ((f32[2,16,4096]{2,0,1:T(2,128)}), f32[2,16,4096]{2,0,1:T(2,128)S(1)}, u32[]{:S(2)}, u32[]{:S(2)}) async-start(f32[2,16,4096]{2,0,1:T(2,128)} %copy.22), calls=%async_computation.1 | async-start | bytes 1048576 | tf_op jit(solution)/shard_map/all_to_all | solution.py:33
  66.0 40.0 %all-reduce.2 = (s32[32]{0:T(128)S(1)}, s32[32]{0:T(128)S(1)}) all-reduce(s32[32]{0:T(128)S(1)} %dynamic-update-slice, s32[32]{0:T(128)S(1)} %dynamic-update-slice.1), channel_id=1, replica_groups=mesh['chip'=2,'board'=4,'cuts'=4] {'chip','board','cuts'}, use_global_device_ids=true, to_apply=%add | all-reduce | flops 64 | bytes 512
  106.0 0.3 copy.23
  106.6 0.4 fusion.47
  107.0 10.5 %all_to_all.21 = f32[2,16,4096]{2,1,0:T(8,128)S(1)} all-to-all(f32[2,16,4096]{2,1,0:T(8,128)S(1)} %bitcast.32), channel_id=1, replica_groups=mesh['chip'=2,'board'=4,'cuts'=4] {'chip'}, dimensions={0} | all-to-all | bytes 1048576 | tf_op jit(solution)/shard_map/all_to_all | solution.py:45
  117.5 1.2 copy.24
  118.7 4.4 %all-to-all-start.3 = ((f32[2,16,4096]{2,0,1:T(2,128)}), f32[2,16,4096]{2,0,1:T(2,128)S(1)}, u32[]{:S(2)}, u32[]{:S(2)}) async-start(f32[2,16,4096]{2,0,1:T(2,128)} %copy.24), calls=%async_computation.3 | async-start | bytes 1048576 | tf_op jit(solution)/shard_map/all_to_all | solution.py:44
  123.3 0.6 dynamic_slice.4
  124.4 13.0 %all-to-all-done.3 = f32[2,16,4096]{2,0,1:T(2,128)S(1)} async-done(((f32[2,16,4096]{2,0,1:T(2,128)}), f32[2,16,4096]{2,0,1:T(2,128)S(1)}, u32[]{:S(2)}, u32[]{:S(2)}) %all-to-all-start.3) | async-done | bytes 524320 | tf_op jit(solution)/shard_map/all_to_all | solution.py:44
  137.4 0.3 copy_divide_fusion
  137.7 0.9 div.20
  (22 shorter events, 0.8 us)
Async XLA Ops:
  0.0 1.3 copy-start
  7.7 7.5 %copy-start.1 = (bf16[1,2048,256]{2,1,0:T(8,128)(2,1)S(1)}, bf16[1,2048,256]{2,1,0:T(8,128)(2,1)}, u32[]{:S(2)}) copy-start(bf16[1,2048,256]{2,1,0:T(8,128)(2,1)} %param.12) | copy-start | bytes 3145732
  27.7 4.0 %copy-start.4 = (f32[1,512,256]{2,1,0:T(8,128)S(1)}, f32[1,512,256]{2,1,0:T(8,128)}, u32[]{:S(2)}) copy-start(f32[1,512,256]{2,1,0:T(8,128)} %param.14) | copy-start | bytes 1572868
  31.7 3.7 %copy-start.2 = (f32[1024,512]{1,0:T(8,128)S(1)}, f32[1024,512]{1,0:T(8,128)}, u32[]{:S(2)}) copy-start(f32[1024,512]{1,0:T(8,128)} %gather_fusion) | copy-start | bytes 6291460
  35.4 4.3 %copy-start.3 = (f32[1024,512]{1,0:T(8,128)S(1)}, f32[1024,512]{1,0:T(8,128)}, u32[]{:S(2)}) copy-start(f32[1024,512]{1,0:T(8,128)} %gather_fusion.2) | copy-start | bytes 6291460
  59.2 46.8 %all-to-all-start.1 = ((f32[2,16,4096]{2,0,1:T(2,128)}), f32[2,16,4096]{2,0,1:T(2,128)S(1)}, u32[]{:S(2)}, u32[]{:S(2)}) async-start(f32[2,16,4096]{2,0,1:T(2,128)} %copy.22), calls=%async_computation.1 | async-start | bytes 1048576 | tf_op jit(solution)/shard_map/all_to_all | solution.py:33
  118.7 18.7 %all-to-all-start.3 = ((f32[2,16,4096]{2,0,1:T(2,128)}), f32[2,16,4096]{2,0,1:T(2,128)S(1)}, u32[]{:S(2)}, u32[]{:S(2)}) async-start(f32[2,16,4096]{2,0,1:T(2,128)} %copy.24), calls=%async_computation.3 | async-start | bytes 1048576 | tf_op jit(solution)/shard_map/all_to_all | solution.py:44
where the time goes:
time: 139 us
  blocking collectives  62.6 us (45%)
  local copies, waits for them, and re-layouts  29.7 us (21%)
  matrix products  20.5 us (15%)
  waiting for transfers between devices  13 us (9%)
  starting transfers between devices  10.4 us (7%)
  between operations  2.04 us (1%)
    unnamed x1, blocking collectives  40 us
    gather x2, local copies, waits for them, and re-layouts, on_device(): picked = jnp.take(hidden, batch_rows[0, step], axis=0)  15 us
    all_to_all x1, waiting for transfers between devices, on_device(): lax.all_to_all(lax.all_to_all(outgoing, 'chip', split_axis=0, concat_axis...  13 us
    all_to_all x1, blocking collectives, on_device(): lax.all_to_all(scaled, 'chip', split_axis=0, concat_axis=0, tiled=True)  12.1 us
    all_to_all x1, blocking collectives, on_device(): lax.all_to_all(outgoing, 'chip', split_axis=0, concat_axis=0, tiled=True)  10.5 us
    gather x2, local copies, waits for them, and re-layouts, on_device(): jnp.take(targets[0], batch_rows[0, step], axis=0).astype(jnp.float32)  8.91 us
    dot_general x2, matrix products, on_device(): grad = jnp.dot(picked.T, err, precision=lax.Precision.HIGHEST) / count_rows  7.26 us
    dot_general x1, matrix products, on_device(): jnp.dot(features[0], lower_weight[0], preferred_element_type=jnp.float32)  6.46 us
  transfers between devices with their start and end apart: 2, of which 1 were waited for; matrix products, arithmetic and copies ran while one was open for 1% of the time, Pallas kernels for 0%

commit v1 on v0

--- a/solution.py
+++ b/solution.py
@@ -4,6 +4,17 @@
 from jax.sharding import PartitionSpec as P
 
 LR = 0.5
+
+
+def pass_leaf(page, peer_axis, at_axis, axis_no):
+    t1 = jax.lax.all_to_all(
+        jnp.stack(jnp.split(page, jax.lax.axis_size(peer_axis), at_axis), 0),
+        axis_name=peer_axis,
+        split_axis=0,
+        concat_axis=0,
+    )
+    taken_in = jnp.concatenate(t1, axis_no)
+    return taken_in
 
 
 def on_device(features, targets, lower_weight, head_weight, batch_rows, sample_counts, cluster_ids):
@@ -41,12 +52,11 @@
     share = jnp.dot(table.T, columns, precision=lax.Precision.HIGHEST)
     outgoing = jnp.dot(table, share, precision=lax.Precision.HIGHEST)
     outgoing = outgoing.reshape(chip_count, rest_count, -1)
-    arrived = lax.all_to_all(
+    arrived = pass_leaf(
         lax.all_to_all(outgoing, "chip", split_axis=0, concat_axis=0, tiled=True),
         ("board", "cuts"),
-        split_axis=1,
-        concat_axis=1,
-        tiled=True,
+        1,
+        1,
     )
     mine = arrived.reshape(delta.shape)
     denom = lax.dynamic_index_in_dim(counts, cluster, 0, keepdims=False)

time: 139 us -> 149 us (1.072)
  local copies, waits for them, and re-layouts: 29.7 us -> 39.2 us
    unnamed x14 -> x29, local copies, waits for them, and re-layouts: 0.65 us -> 10.3 us
where the time goes in v1:
time: 149 us; the launch traced here: 148 us
  blocking collectives  62.6 us (42%)
  local copies, waits for them, and re-layouts  39.2 us (26%)
  matrix products  20.6 us (14%)
  waiting for transfers between devices  12.8 us (9%)
  starting transfers between devices  10.4 us (7%)
  between operations  2.19 us (1%)
    unnamed x1, blocking collectives  39.9 us
    gather x2, local copies, waits for them, and re-layouts, on_device(): picked = jnp.take(hidden, batch_rows[0, step], axis=0)  15.1 us
    all_to_all x1, waiting for transfers between devices, pass_leaf(): jax.lax.all_to_all(jnp.stack(jnp.split(page, jax.lax.axis_size(peer_axis)...  12.8 us
    all_to_all x1, blocking collectives, on_device(): lax.all_to_all(scaled, 'chip', split_axis=0, concat_axis=0, tiled=True)  12.1 us
    all_to_all x1, blocking collectives, on_device(): lax.all_to_all(outgoing, 'chip', split_axis=0, concat_axis=0, tiled=True)  10.5 us
    unnamed x29, local copies, waits for them, and re-layouts  10.3 us
    gather x2, local copies, waits for them, and re-layouts, on_device(): jnp.take(targets[0], batch_rows[0, step], axis=0).astype(jnp.float32)  8.91 us
    dot_general x2, matrix products, on_device(): grad = jnp.dot(picked.T, err, precision=lax.Precision.HIGHEST) / count_rows  7.28 us
  transfers between devices with their start and end apart: 2, of which 1 were waited for; matrix products, arithmetic and copies ran while one was open for 1% of the time, Pallas kernels for 0%

profile of v1, /device:TPU:0, one launch (start us, length us, event | category | flops | bytes accessed | tf_op | source)
XLA Modules:
  0.0 148.3 jit_solution(5060657107381090459)
XLA Ops:
  0.0 0.8 fusion.73
  1.3 6.5 %fusion.2 = f32[2048,512]{1,0:T(8,128)} fusion(bf16[1,2048,1024]{2,1,0:T(8,128)(2,1)} %param.11, bf16[1,1024,512]{2,1,0:T(8,128)(2,1)S(1)} %copy-done), kind=kOutput, calls=%fused_computation.6 | convolution fusion | flops 2147483648 | bytes 9437184 | tf_op jit(solution)/shard_map/dot_general | solution.py:21
  7.7 7.6 %gather_fusion = f32[1024,512]{1,0:T(8,128)} fusion(f32[2048,512]{1,0:T(8,128)} %fusion.2, s32[1024]{0:T(1024)S(1)} %get-tuple-element.11), kind=kCustom, calls=%fused_computation.clone | custom fusion | bytes 4198400 | tf_op jit(solution)/shard_map/jit(_take)/gather | solution.py:26
  15.3 5.0 %gather_fusion.1 = bf16[1024,256]{1,0:T(8,128)(2,1)} fusion(bf16[2048,256]{1,0:T(8,128)(2,1)S(1)} %bitcast.99, s32[1024]{0:T(1024)S(1)} %get-tuple-element.11), kind=kCustom, calls=%fused_computation.1.clone | custom fusion | bytes 1052672 | tf_op jit(solution)/shard_map/jit(_take)/gather | solution.py:27
  20.3 7.5 %gather_fusion.2 = f32[1024,512]{1,0:T(8,128)} fusion(f32[2048,512]{1,0:T(8,128)} %fusion.2, s32[1024]{0:T(1024)S(1)} %get-tuple-element.12), kind=kCustom, calls=%fused_computation.2.clone | custom fusion | bytes 4198400 | tf_op jit(solution)/shard_map/jit(_take)/gather | solution.py:26
  27.8 3.9 %gather_fusion.3 = bf16[1024,256]{1,0:T(8,128)(2,1)S(1)} fusion(bf16[2048,256]{1,0:T(8,128)(2,1)S(1)} %bitcast.100, s32[1024]{0:T(1024)S(1)} %get-tuple-element.12), kind=kCustom, calls=%fused_computation.3.clone | custom fusion | bytes 1052672 | tf_op jit(solution)/shard_map/jit(_take)/gather | solution.py:27
  31.8 3.7 %fusion.13 = f32[1024,256]{1,0:T(8,128)S(1)} fusion(f32[1024,512]{1,0:T(8,128)} %gather_fusion, pred[1024]{0:T(1024)(128)(4,1)S(1)} %compare_and_fusion.1, f32[1,512,256]{2,1,0:T(8,128)S(1)} %copy-done.4, bf16[1024,256]{1,0:T(8,128)(2,1)} %gather_fusion.1), kind=kOutput, calls=%fused_computation.15 | convolution fusion | flops 1611923456 | bytes 4195328 | tf_op jit(solution)/shard_map/dot_general | solution.py:28
  35.5 3.6 %fusion.34 = f32[512,256]{1,0:T(8,128)S(1)} fusion(f32[1024,256]{1,0:T(8,128)S(1)} %fusion.13, f32[1024,512]{1,0:T(8,128)S(1)} %copy-done.2, pred[1024]{0:T(1024)(128)(4,1)S(1)} %compare_and_fusion.1, f32[1,512,256]{2,1,0:T(8,128)S(1)} %copy-done.4), kind=kOutput, calls=%fused_computation.22 | convolution fusion | flops 1611399168 | bytes 4195328 | tf_op jit(solution)/shard_map/dot_general | solution.py:29
  39.8 2.4 %fusion.16 = f32[1024,256]{1,0:T(8,128)S(1)} fusion(f32[512,256]{1,0:T(8,128)S(1)} %fusion.34, f32[1024,512]{1,0:T(8,128)S(1)} %copy-done.3, pred[1024]{0:T(1024)(128)(4,1)S(1)} %compare_and_fusion, bf16[1024,256]{1,0:T(8,128)(2,1)S(1)} %gather_fusion.3), kind=kOutput, calls=%fused_computation.16 | convolution fusion | flops 1611923456 | bytes 4195328 | tf_op jit(solution)/shard_map/dot_general | solution.py:28
  42.2 3.6 %fusion.31 = f32[512,256]{1,0:T(8,128)S(1)} fusion(f32[512,256]{1,0:T(8,128)S(1)} %fusion.34, f32[1024,256]{1,0:T(8,128)S(1)} %fusion.16, f32[1024,512]{1,0:T(8,128)S(1)} %copy-done.3, pred[1024]{0:T(1024)(128)(4,1)S(1)} %compare_and_fusion, f32[1,512,256]{2,1,0:T(8,128)S(1)} %copy-done.4, f32[]{:T(128)} %bitcast), kind=kOutput, calls=%fused_computation.21 | convolution fusion | flops 1611661312 | bytes 4719620 | tf_op jit(solution)/shard_map/dot_general | solution.py:29
  45.9 12.1 %all_to_all.20 = f32[2,16,4096]{2,1,0:T(8,128)S(1)} all-to-all(f32[2,16,4096]{2,1,0:T(8,128)S(1)} %reshape.37), channel_id=1, replica_groups=mesh['chip'=2,'board'=4,'cuts'=4] {'chip'}, dimensions={0} | all-to-all | bytes 1048576 | tf_op jit(solution)/shard_map/all_to_all | solution.py:45
  58.1 1.2 copy.17
  59.3 5.9 %all-to-all-start.1 = ((f32[2,16,4096]{2,0,1:T(2,128)}), f32[2,16,4096]{2,0,1:T(2,128)S(1)}, u32[]{:S(2)}, u32[]{:S(2)}) async-start(f32[2,16,4096]{2,0,1:T(2,128)} %copy.17), calls=%async_computation.1 | async-start | bytes 1048576 | tf_op jit(solution)/shard_map/all_to_all | solution.py:44
  66.1 39.9 %all-reduce.2 = (s32[32]{0:T(128)S(1)}, s32[32]{0:T(128)S(1)}) all-reduce(s32[32]{0:T(128)S(1)} %dynamic-update-slice, s32[32]{0:T(128)S(1)} %dynamic-update-slice.1), channel_id=1, replica_groups=mesh['chip'=2,'board'=4,'cuts'=4] {'chip','board','cuts'}, use_global_device_ids=true, to_apply=%add | all-reduce | flops 64 | bytes 512
  107.1 10.5 %all_to_all.21 = f32[2,16,4096]{2,1,0:T(8,128)S(1)} all-to-all(f32[2,16,4096]{2,1,0:T(8,128)S(1)} %bitcast.102), channel_id=1, replica_groups=mesh['chip'=2,'board'=4,'cuts'=4] {'chip'}, dimensions={0} | all-to-all | bytes 1048576 | tf_op jit(solution)/shard_map/all_to_all | solution.py:56
  118.2 0.6 fusion.61
  118.9 0.6 fusion.60
  119.5 0.6 fusion.59
  120.1 0.6 fusion.58
  121.4 0.6 fusion.56
  127.9 4.4 %all-to-all-start.3 = ((f32[16,2,1,4096]{3,2,1,0:T(1,128)}), f32[16,2,1,4096]{3,2,1,0:T(1,128)S(1)}, u32[]{:S(2)}, u32[]{:S(2)}) async-start(f32[16,2,1,4096]{3,2,1,0:T(1,128)} %fusion.47), calls=%async_computation.3 | async-start | bytes 1048576 | tf_op jit(solution)/shard_map/all_to_all | solution.py:10
  132.4 0.7 dynamic_slice.4
  133.8 12.8 %all-to-all-done.3 = f32[16,2,1,4096]{3,2,1,0:T(1,128)S(1)} async-done(((f32[16,2,1,4096]{3,2,1,0:T(1,128)}), f32[16,2,1,4096]{3,2,1,0:T(1,128)S(1)}, u32[]{:S(2)}, u32[]{:S(2)}) %all-to-all-start.3) | async-done | bytes 524320 | tf_op jit(solution)/shard_map/all_to_all | solution.py:10
  147.4 0.9 div.24
  (37 shorter events, 9.7 us)
Async XLA Ops:
  0.0 1.3 copy-start
  7.7 7.6 %copy-start.1 = (bf16[1,2048,256]{2,1,0:T(8,128)(2,1)S(1)}, bf16[1,2048,256]{2,1,0:T(8,128)(2,1)}, u32[]{:S(2)}) copy-start(bf16[1,2048,256]{2,1,0:T(8,128)(2,1)} %param.12) | copy-start | bytes 3145732
  27.8 4.0 %copy-start.4 = (f32[1,512,256]{2,1,0:T(8,128)S(1)}, f32[1,512,256]{2,1,0:T(8,128)}, u32[]{:S(2)}) copy-start(f32[1,512,256]{2,1,0:T(8,128)} %param.14) | copy-start | bytes 1572868
  31.7 3.7 %copy-start.2 = (f32[1024,512]{1,0:T(8,128)S(1)}, f32[1024,512]{1,0:T(8,128)}, u32[]{:S(2)}) copy-start(f32[1024,512]{1,0:T(8,128)} %gather_fusion) | copy-start | bytes 6291460
  35.4 4.3 %copy-start.3 = (f32[1024,512]{1,0:T(8,128)S(1)}, f32[1024,512]{1,0:T(8,128)}, u32[]{:S(2)}) copy-start(f32[1024,512]{1,0:T(8,128)} %gather_fusion.2) | copy-start | bytes 6291460
  59.3 46.8 %all-to-all-start.1 = ((f32[2,16,4096]{2,0,1:T(2,128)}), f32[2,16,4096]{2,0,1:T(2,128)S(1)}, u32[]{:S(2)}, u32[]{:S(2)}) async-start(f32[2,16,4096]{2,0,1:T(2,128)} %copy.17), calls=%async_computation.1 | async-start | bytes 1048576 | tf_op jit(solution)/shard_map/all_to_all | solution.py:44
  127.9 18.7 %all-to-all-start.3 = ((f32[16,2,1,4096]{3,2,1,0:T(1,128)}), f32[16,2,1,4096]{3,2,1,0:T(1,128)S(1)}, u32[]{:S(2)}, u32[]{:S(2)}) async-start(f32[16,2,1,4096]{3,2,1,0:T(1,128)} %fusion.47), calls=%async_computation.3 | async-start | bytes 1048576 | tf_op jit(solution)/shard_map/all_to_all | solution.py:10
